TPU v7x, 32 devices: a whole 2x2x4 slice. The times are simulated.
32 devices in a mesh: node: 8 (over y, x, core), grp: 4 (over z).
Axes of the slice: x: 2, y: 2, z: 4, core: 2. Of those that a mesh axis runs over, the one named last changes fastest.
Arguments:
- tokens: bfloat16 [12288, 1792], P(('node', 'grp')), may hold values from -6 to 6
- cotangent: bfloat16 [12288, 1792], P(('node', 'grp')), may hold values from -6 to 6
- gate_weight: bfloat16 [1792, 1024], P('node'), may hold values from -0.125 to 0.125
- up_weight: bfloat16 [1792, 1024], P('node'), may hold values from -0.125 to 0.125
- down_weight_t: bfloat16 [1792, 1024], P('node'), may hold values from -0.125 to 0.125
- error_memory: bfloat16 [4, 1792, 3072], P('grp', 'node'), may hold values from -4 to 4
- q_init: float32 [3, 1024, 32], replicated, may hold values from -6 to 6
Outputs:
- token_grad: bfloat16 [12288, 1792], P(('node', 'grp'))
- new_error: bfloat16 [4, 1792, 3072], P('grp', 'node')
- p_hat: float32 [3, 1792, 32], P(None, 'node')
- q_new: float32 [3, 1024, 32], replicated
All inputs are finite; a program needn't handle non-finite values.
Results may differ from a plain program's by a relative error of at most 0.012.
Values may be sent and summed in bfloat16 or wider, within the bound.
A program may use at most 192 MiB of HBM per device.

v0:
```python
import math
import jax
import jax.numpy as jnp
from jax import lax
from jax.sharding import PartitionSpec as P


def gelu_parts(value):
    coeff = math.sqrt(2.0 / math.pi)
    inner = coeff * (value + 0.044715 * value * value * value)
    tanh_value = jnp.tanh(inner)
    activation = 0.5 * value * (1.0 + tanh_value)
    slope = 0.5 * (1.0 + tanh_value) + 0.5 * value * (1.0 - tanh_value * tanh_value) * coeff * (
        1.0 + 3.0 * 0.044715 * value * value
    )
    return (activation, slope)


def contract_rows(left_side, right_side):
    return lax.dot_general(
        left_side, right_side, (((0,), (0,)), ((), ())), preferred_element_type=jnp.float32
    )


def on_device(tokens, cotangent, gate_weight, up_weight, down_weight_t, error_memory, q_init):
    node_count = lax.axis_size("node")
    group_count = lax.axis_size("grp")
    hidden_units = gate_weight.shape[1]
    highest = lax.Precision.HIGHEST
    full_gate, full_up, full_down = (
        lax.all_gather(gate_weight, "node", axis=0, tiled=True),
        lax.all_gather(up_weight, "node", axis=0, tiled=True),
        lax.all_gather(down_weight_t, "node", axis=0, tiled=True),
    )
    gate_pre = jnp.dot(tokens, full_gate, preferred_element_type=jnp.float32)
    up_pre = jnp.dot(tokens, full_up, preferred_element_type=jnp.float32)
    activation, slope = gelu_parts(gate_pre)
    hidden = (activation * up_pre).astype(jnp.bfloat16)
    back_hidden = jnp.dot(cotangent, full_down, preferred_element_type=jnp.float32)
    grad_up = (back_hidden * activation).astype(jnp.bfloat16)
    grad_gate = (back_hidden * up_pre * slope).astype(jnp.bfloat16)
    token_grad = (
        lax.dot_general(
            grad_gate, full_gate, (((1,), (1,)), ((), ())), preferred_element_type=jnp.float32
        )
        + lax.dot_general(
            grad_up, full_up, (((1,), (1,)), ((), ())), preferred_element_type=jnp.float32
        )
    ).astype(jnp.bfloat16)
    gate_up = jnp.concatenate([grad_gate, grad_up], axis=1)
    token_cols, cot_cols = (
        lax.all_to_all(tokens, "node", split_axis=1, concat_axis=0, tiled=True),
        lax.all_to_all(cotangent, "node", split_axis=1, concat_axis=0, tiled=True),
    )
    piece_gu = lax.all_gather(gate_up, "node", axis=0, tiled=True)
    piece_hidden = lax.all_gather(hidden, "node", axis=0, tiled=True)
    summed = jnp.concatenate(
        [contract_rows(token_cols, piece_gu), contract_rows(cot_cols, piece_hidden)], axis=1
    )
    grad_scale = 1.0 / math.sqrt(tokens.shape[0] * node_count)
    merged = summed * grad_scale + error_memory[0].astype(jnp.float32)
    blocks = [merged[:, m * hidden_units : (m + 1) * hidden_units] for m in range(3)]
    row_terms = jnp.stack([jnp.dot(blocks[m], q_init[m], precision=highest) for m in range(3)])
    power_rows = lax.psum(row_terms.astype(jnp.bfloat16), "grp").astype(jnp.float32) / group_count
    local_gram = jnp.einsum("mdr,mds->mrs", power_rows, power_rows, precision=highest)
    gram_matrix = lax.psum(local_gram, "node")
    hats = []
    for m in range(3):
        factor = jnp.linalg.cholesky(gram_matrix[m])
        hats.append(jax.scipy.linalg.solve_triangular(factor, power_rows[m].T, lower=True).T)
    col_terms = jnp.stack([jnp.dot(blocks[m].T, hats[m], precision=highest) for m in range(3)])
    q_new = lax.psum(col_terms, ("node", "grp")) / group_count
    errors = [blocks[m] - jnp.dot(hats[m], q_new[m].T, precision=highest) for m in range(3)]
    new_error = jnp.concatenate(errors, axis=1).astype(jnp.bfloat16)[None]
    return (token_grad, new_error, jnp.stack(hats), q_new)


def solution(mesh):
    return jax.shard_map(
        on_device,
        mesh=mesh,
        in_specs=(
            P(("node", "grp"), None),
            P(("node", "grp"), None),
            P("node", None),
            P("node", None),
            P("node", None),
            P("grp", "node", None),
            P(),
        ),
        out_specs=(P(("node", "grp"), None), P("grp", "node", None), P(None, "node", None), P()),
        check_vma=False,
    )
```

profile of v0, /device:TPU:0, one launch (start us, length us, event | category | flops | bytes accessed | tf_op | source)
XLA Modules:
  0.0 512.1 jit_solution(15546751805123783097)
XLA Ops:
  9.4 37.6 %all-gather.6.cloned.1.call-done = bf16[1792,1024]{1,0:T(8,128)(2,1)} async-done(((bf16[224,1024]{1,0:T(8,128)(2,1)}), bf16[1792,1024]{1,0:T(8,128)(2,1)}) %all-gather.6.cloned.1.call-update) | async-done | bytes 3670032 | tf_op jit(solution)/shard_map/all_gather | solution.py:33
  47.0 5.2 %fusion.44 = f32[384,1024]{1,0:T(8,128)} fusion(bf16[384,1792]{1,0:T(8,128)(2,1)} %param.11, bf16[1792,1024]{1,0:T(8,128)(2,1)} %all-gather.6.cloned.1.call-done), kind=kOutput, calls=%fused_computation.92 | convolution fusion | flops 1409286144 | bytes 6619136 | tf_op jit(solution)/shard_map/dot_general | solution.py:39
  52.2 31.1 %all-gather.10.cloned.1.call-done = bf16[1792,1024]{1,0:T(8,128)(2,1)} async-done(((bf16[224,1024]{1,0:T(8,128)(2,1)}), bf16[1792,1024]{1,0:T(8,128)(2,1)}) %all-gather.10.cloned.1.call-update) | async-done | bytes 3670032 | tf_op jit(solution)/shard_map/all_gather | solution.py:31
  83.3 4.8 fusion.45
  88.1 31.5 %all-gather.8.cloned.1.call-done = bf16[1792,1024]{1,0:T(8,128)(2,1)} async-done(((bf16[224,1024]{1,0:T(8,128)(2,1)}), bf16[1792,1024]{1,0:T(8,128)(2,1)}) %all-gather.8.cloned.1.call-update) | async-done | bytes 3670032 | tf_op jit(solution)/shard_map/all_gather | solution.py:32
  119.6 6.4 %multiply_convert_fusion = (bf16[384,1024]{1,0:T(8,128)(2,1)}, bf16[384,1024]{1,0:T(8,128)(2,1)S(1)}, bf16[384,1024]{1,0:T(8,128)(2,1)S(1)}) fusion(f32[384,1024]{1,0:T(8,128)} %fusion.45, f32[384,1024]{1,0:T(8,128)} %fusion.44, bf16[384,1792]{1,0:T(8,128)(2,1)S(1)} %copy-done.2, bf16[1792,1024]{1,0:T(8,128)(2,1)} %all-gather.8.cloned.1.call-done), kind=kOutput, calls=%fused_computation.15 | convolution fusion | flops 1419116544 | bytes 10551296 | tf_op jit(solution)/shard_map/dot_general | solution.py:36
  126.9 1.4 pad_maximum_fusion
  128.3 1.3 copy-done.1
  129.6 1.5 copy.17
  131.1 3.6 all-to-all-start.1
  134.7 1.5 copy.15
  136.3 24.3 %all-to-all-done.1 = bf16[384,8,224]{0,2,1:T(8,128)(2,1)S(1)} async-done(((bf16[384,8,224]{0,2,1:T(8,128)(2,1)}), bf16[384,8,224]{0,2,1:T(8,128)(2,1)S(1)}, u32[]{:S(2)}, u32[]{:S(2)}) %all-to-all-start.1) | async-done | bytes 1376288 | tf_op jit(solution)/shard_map/all_to_all | solution.py:53
  160.5 3.6 all-to-all-start
  164.3 1.3 copy.25
  165.7 31.9 %all-to-all-done = bf16[384,8,224]{0,2,1:T(8,128)(2,1)S(1)} async-done(((bf16[384,8,224]{0,2,1:T(8,128)(2,1)}), bf16[384,8,224]{0,2,1:T(8,128)(2,1)S(1)}, u32[]{:S(2)}, u32[]{:S(2)}) %all-to-all-start) | async-done | bytes 1376288 | tf_op jit(solution)/shard_map/all_to_all | solution.py:52
  197.6 1.3 copy.24
  198.9 5.4 %fusion.46 = f32[384,1792]{1,0:T(8,128)} fusion(bf16[384,1024]{1,0:T(8,128)(2,1)S(1)} %copy-done.8, bf16[1792,1024]{1,0:T(8,128)(2,1)} %all-gather.10.cloned.1.call-done), kind=kOutput, calls=%fused_computation.94 | convolution fusion | flops 1409286144 | bytes 7208960 | tf_op jit(solution)/shard_map/dot_general | solution.py:43
  204.3 5.4 %convolution_bitcast_fusion.1 = f32[224,1024]{1,0:T(8,128)} fusion(bf16[3072,224]{0,1:T(8,128)(2,1)S(1)} %bitcast.133, bf16[3072,1024]{1,0:T(8,128)(2,1)} %all-gather.14.cloned.1.call-done), kind=kOutput, calls=%fused_computation.19 | convolution fusion | flops 1409286144 | bytes 8585216 | tf_op jit(solution)/shard_map/dot_general | solution.py:20
  209.7 64.7 %all-gather.12.cloned.1.call-done = bf16[3072,2048]{1,0:T(8,128)(2,1)} async-done(((bf16[384,2048]{1,0:T(8,128)(2,1)}), bf16[3072,2048]{1,0:T(8,128)(2,1)}) %all-gather.12.cloned.1.call-update) | async-done | bytes 12582928 | tf_op jit(solution)/shard_map/all_gather | solution.py:55
  274.4 6.4 %convolution_bitcast_fusion = f32[224,2048]{1,0:T(8,128)S(1)} fusion(bf16[3072,224]{0,1:T(8,128)(2,1)S(1)} %bitcast.134, bf16[3072,2048]{1,0:T(8,128)(2,1)} %all-gather.12.cloned.1.call-done), kind=kOutput, calls=%fused_computation.4 | convolution fusion | flops 2818572288 | bytes 15794176 | tf_op jit(solution)/shard_map/dot_general | solution.py:20
  285.2 20.5 %psum.21 = bf16[3,224,32]{1,2,0:T(8,128)(2,1)} all-reduce(bf16[3,224,32]{1,2,0:T(8,128)(2,1)} %pad_maximum_fusion.4), channel_id=1, replica_groups=mesh['node'=8,'grp'=4] {'grp'}, use_global_device_ids=true, to_apply=%region_0.0 | all-reduce | flops 21504 | bytes 86016 | tf_op jit(solution)/shard_map/psum | solution.py:64
  305.6 1.7 fusion.33
  307.4 1.4 convert_multiply_fusion
  308.8 24.0 %psum.22 = f32[3,32,32]{1,2,0:T(8,128)} all-reduce(f32[3,32,32]{1,2,0:T(8,128)} %fusion.33), channel_id=1, replica_groups=mesh['node'=8,'grp'=4] {'node'}, use_global_device_ids=true, to_apply=%region_1.0 | all-reduce | flops 3072 | bytes 24576 | tf_op jit(solution)/shard_map/psum | solution.py:66
  332.9 1.4 slice_bitcast_fusion.14
  335.0 1.4 copy.22
  336.4 1.4 copy.21
  337.8 1.4 fusion.39
  339.2 3.6 cholesky.59
  343.5 1.3 fusion.34
  344.8 3.8 custom-call.7
  348.5 3.6 cholesky.70
  352.9 1.3 fusion.35
  354.1 3.2 custom-call.8
  357.3 1.6 fusion.32
  358.9 1.6 fusion.31
  360.5 3.6 cholesky.81
  364.8 1.3 fusion.36
  366.0 3.2 custom-call.9
  369.2 1.0 fusion.30
  370.9 1.4 convolution_bitcast_fusion.3
  373.8 5.7 %fusion = bf16[384,1792]{1,0:T(8,128)(2,1)} fusion(f32[384,1792]{1,0:T(8,128)} %fusion.46, bf16[384,1024]{1,0:T(8,128)(2,1)S(1)} %get-tuple-element.8, bf16[1792,1024]{1,0:T(8,128)(2,1)} %all-gather.8.cloned.1.call-done), kind=kOutput, calls=%fused_computation.1 | convolution fusion | flops 1410662400 | bytes 8585216 | tf_op jit(solution)/shard_map/dot_general | solution.py:46
  380.2 119.2 %all-reduce.2.cloned.1.call-done = f32[3,1024,32]{1,2,0:T(8,128)} async-done(((f32[3,1024,32]{1,2,0:T(8,128)}), f32[3,1024,32]{1,2,0:T(8,128)}) %all-reduce.2.cloned.1.call-update) | async-done | bytes 393232 | tf_op jit(solution)/shard_map/psum | solution.py:72
  499.4 1.0 broadcast_multiply_fusion
  500.4 1.8 fusion.12
  502.2 0.9 fusion.13
  503.1 0.9 fusion.14
  504.1 1.2 pad_maximum_fusion.1
  (62 shorter events, 13.3 us)
Async XLA Ops:
  7.2 39.8 %all-gather.6.cloned.1.call-start = ((), (), s32[]{:S(2)}) async-start(), calls=%async_computation.2 | async-start | bytes 4128768 | tf_op jit(solution)/shard_map/all_gather | solution.py:33
  7.9 75.4 %all-gather.10.cloned.1.call-start = ((), (), s32[]{:S(2)}) async-start(), calls=%async_computation.4 | async-start | bytes 4128768 | tf_op jit(solution)/shard_map/all_gather | solution.py:31
  8.6 111.0 %all-gather.8.cloned.1.call-start = ((), (), s32[]{:S(2)}) async-start(), calls=%async_computation.3 | async-start | bytes 4128768 | tf_op jit(solution)/shard_map/all_gather | solution.py:32
  9.4 73.9 %copy-start.2 = (bf16[384,1792]{1,0:T(8,128)(2,1)S(1)}, bf16[384,1792]{1,0:T(8,128)(2,1)}, u32[]{:S(2)}) copy-start(bf16[384,1792]{1,0:T(8,128)(2,1)} %param.10) | copy-start | bytes 4128772
  9.4 194.9 %all-gather.14.cloned.1.call-start = ((), (), s32[]{:S(2)}) async-start(), calls=%async_computation.6 | async-start | bytes 7077888 | tf_op jit(solution)/shard_map/all_gather | solution.py:56
  126.0 0.9 copy-start.7
  126.0 148.4 %all-gather.12.cloned.1.call-start = ((), (), s32[]{:S(2)}) async-start(), calls=%async_computation.5 | async-start | bytes 14155776 | tf_op jit(solution)/shard_map/all_gather | solution.py:55
  128.2 1.3 copy-start.1
  131.1 29.4 %all-to-all-start.1 = ((bf16[384,8,224]{0,2,1:T(8,128)(2,1)}), bf16[384,8,224]{0,2,1:T(8,128)(2,1)S(1)}, u32[]{:S(2)}, u32[]{:S(2)}) async-start(bf16[384,8,224]{0,2,1:T(8,128)(2,1)} %bitcast.3), calls=%async_computation.1 | async-start | bytes 2752512 | tf_op jit(solution)/shard_map/all_to_all | solution.py:53
  160.5 37.1 %all-to-all-start = ((bf16[384,8,224]{0,2,1:T(8,128)(2,1)}), bf16[384,8,224]{0,2,1:T(8,128)(2,1)S(1)}, u32[]{:S(2)}, u32[]{:S(2)}) async-start(bf16[384,8,224]{0,2,1:T(8,128)(2,1)} %bitcast), calls=%async_computation | async-start | bytes 2752512 | tf_op jit(solution)/shard_map/all_to_all | solution.py:52
  164.1 335.3 %all-reduce.2.cloned.1.call-start = ((), (), s32[]{:S(2)}) async-start(), calls=%async_computation.7 | async-start | bytes 786432 | tf_op jit(solution)/shard_map/psum | solution.py:72
  197.6 1.3 copy-start.8
  198.9 5.4 %copy-start.4 = (bf16[8,28,8,384]{3,2,0,1:T(8,128)(2,1)S(1)}, bf16[8,28,8,384]{3,2,0,1:T(8,128)(2,1)}, u32[]{:S(2)}) copy-start(bf16[8,28,8,384]{3,2,0,1:T(8,128)(2,1)} %copy.25) | copy-start | bytes 4128772
  204.3 70.1 %copy-start.5 = (bf16[8,28,8,384]{3,2,0,1:T(8,128)(2,1)S(1)}, bf16[8,28,8,384]{3,2,0,1:T(8,128)(2,1)}, u32[]{:S(2)}) copy-start(bf16[8,28,8,384]{3,2,0,1:T(8,128)(2,1)} %copy.24) | copy-start | bytes 4128772
  274.4 6.4 %copy-start.3 = (bf16[1,224,3072]{2,1,0:T(8,128)(2,1)S(1)}, bf16[1,224,3072]{2,1,0:T(8,128)(2,1)}, u32[]{:S(2)}) copy-start(bf16[1,224,3072]{2,1,0:T(8,128)(2,1)} %param.15) | copy-start | bytes 4128772
  274.4 6.4 %copy-start.6 = (f32[224,1024]{1,0:T(8,128)S(1)}, f32[224,1024]{1,0:T(8,128)}, u32[]{:S(2)}) copy-start(f32[224,1024]{1,0:T(8,128)} %convolution_bitcast_fusion.1) | copy-start | bytes 2752516
  280.8 1.0 copy-start.16
  369.2 3.1 copy-start.9
  370.2 2.8 copy-start.14
  373.8 5.7 %copy-start.10 = (f32[32,224]{1,0:T(8,128)S(1)}, f32[32,224]{1,0:T(8,128)}, u32[]{:S(2)}) copy-start(f32[32,224]{1,0:T(8,128)} %fusion.32) | copy-start | bytes 86020
  373.8 5.7 %copy-start.12 = (f32[32,224]{1,0:T(8,128)S(1)}, f32[32,224]{1,0:T(8,128)}, u32[]{:S(2)}) copy-start(f32[32,224]{1,0:T(8,128)} %fusion.31) | copy-start | bytes 86020
  373.8 5.7 %copy-start.15 = (f32[32,224]{1,0:T(8,128)S(1)}, f32[32,224]{1,0:T(8,128)}, u32[]{:S(2)}) copy-start(f32[32,224]{1,0:T(8,128)} %copy-done.14) | copy-start | bytes 86020
  379.5 122.7 %copy-start.13 = (f32[32,224]{1,0:T(8,128)S(1)}, f32[32,224]{1,0:T(8,128)}, u32[]{:S(2)}) copy-start(f32[32,224]{1,0:T(8,128)} %fusion.31) | copy-start | bytes 86020
  500.4 3.7 copy-start
  500.4 2.7 copy-start.11
Sparse Core Ops, SparseCore 0:
  9.9 37.0 all-gather.5
  48.9 34.3 all-gather.9
  85.2 34.3 all-gather.7
  126.1 74.4 all-gather.13
  202.4 71.9 all-gather.11
  373.9 125.4 all-reduce.1
where the time goes:
time: 514 us; the launch traced here: 512 us
  waiting for transfers between devices  342 us (67%)
  matrix products  54.2 us (11%)
  blocking collectives  44.5 us (9%)
  other arithmetic  35.7 us (7%)
  between operations  14.4 us (3%)
  local copies, waits for them, and re-layouts  13.4 us (3%)
  starting transfers between devices  7.6 us (1%)
    psum x1, waiting for transfers between devices, on_device(): q_new = lax.psum(col_terms, ('node', 'grp')) / group_count  119 us
    all_gather x1, waiting for transfers between devices, on_device(): piece_gu = lax.all_gather(gate_up, 'node', axis=0, tiled=True)  64.7 us
    all_gather x1, waiting for transfers between devices, on_device(): lax.all_gather(down_weight_t, 'node', axis=0, tiled=True)  37.6 us
    all_to_all x1, waiting for transfers between devices, on_device(): lax.all_to_all(tokens, 'node', split_axis=1, concat_axis=0, tiled=True)  31.9 us
    all_gather x1, waiting for transfers between devices, on_device(): lax.all_gather(up_weight, 'node', axis=0, tiled=True)  31.5 us
    all_gather x1, waiting for transfers between devices, on_device(): lax.all_gather(gate_weight, 'node', axis=0, tiled=True)  31.1 us
    all_to_all x1, waiting for transfers between devices, on_device(): lax.all_to_all(cotangent, 'node', split_axis=1, concat_axis=0, tiled=True)  24.3 us
    psum x1, blocking collectives, on_device(): gram_matrix = lax.psum(local_gram, 'node')  24 us
  transfers between devices with their start and end apart: 8, of which 7 were waited for; matrix products, arithmetic and copies ran while one was open for 7% of the time, Pallas kernels for 0%

commit v1 on v0

--- a/solution.py
+++ b/solution.py
@@ -69,7 +69,7 @@
         factor = jnp.linalg.cholesky(gram_matrix[m])
         hats.append(jax.scipy.linalg.solve_triangular(factor, power_rows[m].T, lower=True).T)
     col_terms = jnp.stack([jnp.dot(blocks[m].T, hats[m], precision=highest) for m in range(3)])
-    q_new = lax.psum(col_terms, ("node", "grp")) / group_count
+    q_new = jnp.sum(lax.all_gather(col_terms, ("node", "grp")), axis=0) / group_count
     errors = [blocks[m] - jnp.dot(hats[m], q_new[m].T, precision=highest) for m in range(3)]
     new_error = jnp.concatenate(errors, axis=1).astype(jnp.bfloat16)[None]
     return (token_grad, new_error, jnp.stack(hats), q_new)

time: 514 us -> 485 us (0.944)
  waiting for transfers between devices: 342 us -> 313 us
    psum x1 -> x0, waiting for transfers between devices: 119 us -> none  [on_device(): q_new = lax.psum(col_terms, ('node', 'grp')) / group_count]
    all_gather x0 -> x1, waiting for transfers between devices: none -> 84.6 us  [on_device(): lax.all_gather(col_terms, ('node', 'grp'))]
    reduce_sum x0 -> x1, other arithmetic: none -> 5.72 us  [on_device(): jnp.sum(lax.all_gather(col_terms, ('node', 'grp')), axis=0) / group_count]
  transfers between devices with their start and end apart: 8 -> 8, of which waited for: 7 -> 8; matrix products, arithmetic and copies ran while one was open for 7% -> 6% of each run, Pallas kernels for 0% -> 0%
where the time goes in v1:
time: 485 us; the launch traced here: 483 us
  waiting for transfers between devices  313 us (65%)
  matrix products  49.9 us (10%)
  blocking collectives  44.5 us (9%)
  other arithmetic  40.3 us (8%)
  between operations  14.4 us (3%)
  local copies, waits for them, and re-layouts  13.4 us (3%)
  starting transfers between devices  7.42 us (2%)
    all_gather x1, waiting for transfers between devices, on_device(): lax.all_gather(col_terms, ('node', 'grp'))  84.6 us
    all_gather x1, waiting for transfers between devices, on_device(): piece_gu = lax.all_gather(gate_up, 'node', axis=0, tiled=True)  68.4 us
    all_gather x1, waiting for transfers between devices, on_device(): lax.all_gather(down_weight_t, 'node', axis=0, tiled=True)  37.6 us
    all_to_all x1, waiting for transfers between devices, on_device(): lax.all_to_all(tokens, 'node', split_axis=1, concat_axis=0, tiled=True)  32.1 us
    all_gather x1, waiting for transfers between devices, on_device(): lax.all_gather(up_weight, 'node', axis=0, tiled=True)  31.5 us
    all_gather x1, waiting for transfers between devices, on_device(): lax.all_gather(gate_weight, 'node', axis=0, tiled=True)  31.1 us
    all_to_all x1, waiting for transfers between devices, on_device(): lax.all_to_all(cotangent, 'node', split_axis=1, concat_axis=0, tiled=True)  24.4 us
    psum x1, blocking collectives, on_device(): gram_matrix = lax.psum(local_gram, 'node')  24 us
  transfers between devices with their start and end apart: 8, of which 8 were waited for; matrix products, arithmetic and copies ran while one was open for 6% of the time, Pallas kernels for 0%

profile of v1, /device:TPU:0, one launch (start us, length us, event | category | flops | bytes accessed | tf_op | source)
XLA Modules:
  0.0 483.3 jit_solution(10899177169602629110)
XLA Ops:
  9.4 37.6 %all-gather.8.cloned.1.call-done = bf16[1792,1024]{1,0:T(8,128)(2,1)} async-done(((bf16[224,1024]{1,0:T(8,128)(2,1)}), bf16[1792,1024]{1,0:T(8,128)(2,1)}) %all-gather.8.cloned.1.call-update) | async-done | bytes 3670032 | tf_op jit(solution)/shard_map/all_gather | solution.py:33
  47.0 5.2 %fusion.44 = f32[384,1024]{1,0:T(8,128)} fusion(bf16[384,1792]{1,0:T(8,128)(2,1)} %param.11, bf16[1792,1024]{1,0:T(8,128)(2,1)} %all-gather.8.cloned.1.call-done), kind=kOutput, calls=%fused_computation.92 | convolution fusion | flops 1409286144 | bytes 6619136 | tf_op jit(solution)/shard_map/dot_general | solution.py:39
  52.2 31.1 %all-gather.12.cloned.1.call-done = bf16[1792,1024]{1,0:T(8,128)(2,1)} async-done(((bf16[224,1024]{1,0:T(8,128)(2,1)}), bf16[1792,1024]{1,0:T(8,128)(2,1)}) %all-gather.12.cloned.1.call-update) | async-done | bytes 3670032 | tf_op jit(solution)/shard_map/all_gather | solution.py:31
  83.3 4.8 fusion.45
  88.1 31.5 %all-gather.10.cloned.1.call-done = bf16[1792,1024]{1,0:T(8,128)(2,1)} async-done(((bf16[224,1024]{1,0:T(8,128)(2,1)}), bf16[1792,1024]{1,0:T(8,128)(2,1)}) %all-gather.10.cloned.1.call-update) | async-done | bytes 3670032 | tf_op jit(solution)/shard_map/all_gather | solution.py:32
  119.6 6.4 %multiply_convert_fusion = (bf16[384,1024]{1,0:T(8,128)(2,1)}, bf16[384,1024]{1,0:T(8,128)(2,1)S(1)}, bf16[384,1024]{1,0:T(8,128)(2,1)S(1)}) fusion(f32[384,1024]{1,0:T(8,128)} %fusion.45, f32[384,1024]{1,0:T(8,128)} %fusion.44, bf16[384,1792]{1,0:T(8,128)(2,1)S(1)} %copy-done.2, bf16[1792,1024]{1,0:T(8,128)(2,1)} %all-gather.10.cloned.1.call-done), kind=kOutput, calls=%fused_computation.15 | convolution fusion | flops 1419116544 | bytes 10551296 | tf_op jit(solution)/shard_map/dot_general | solution.py:36
  126.8 1.3 pad_maximum_fusion
  128.1 1.3 copy-done.1
  129.5 1.5 copy.25
  131.0 3.6 all-to-all-start.1
  134.6 1.5 copy.23
  136.1 24.4 %all-to-all-done.1 = bf16[384,8,224]{0,2,1:T(8,128)(2,1)S(1)} async-done(((bf16[384,8,224]{0,2,1:T(8,128)(2,1)}), bf16[384,8,224]{0,2,1:T(8,128)(2,1)S(1)}, u32[]{:S(2)}, u32[]{:S(2)}) %all-to-all-start.1) | async-done | bytes 1376288 | tf_op jit(solution)/shard_map/all_to_all | solution.py:53
  160.5 3.6 all-to-all-start
  164.1 1.3 copy.33
  165.5 32.1 %all-to-all-done = bf16[384,8,224]{0,2,1:T(8,128)(2,1)S(1)} async-done(((bf16[384,8,224]{0,2,1:T(8,128)(2,1)}), bf16[384,8,224]{0,2,1:T(8,128)(2,1)S(1)}, u32[]{:S(2)}, u32[]{:S(2)}) %all-to-all-start) | async-done | bytes 1376288 | tf_op jit(solution)/shard_map/all_to_all | solution.py:52
  197.6 1.3 copy.32
  198.9 1.8 all-gather.16.cloned.1.call-done
  200.7 5.4 %convolution_bitcast_fusion.1 = f32[224,1024]{1,0:T(8,128)} fusion(bf16[3072,224]{0,1:T(8,128)(2,1)S(1)} %bitcast.135, bf16[3072,1024]{1,0:T(8,128)(2,1)} %all-gather.16.cloned.1.call-done), kind=kOutput, calls=%fused_computation.19 | convolution fusion | flops 1409286144 | bytes 8585216 | tf_op jit(solution)/shard_map/dot_general | solution.py:20
  206.1 68.4 %all-gather.14.cloned.1.call-done = bf16[3072,2048]{1,0:T(8,128)(2,1)} async-done(((bf16[384,2048]{1,0:T(8,128)(2,1)}), bf16[3072,2048]{1,0:T(8,128)(2,1)}) %all-gather.14.cloned.1.call-update) | async-done | bytes 12582928 | tf_op jit(solution)/shard_map/all_gather | solution.py:55
  274.4 6.4 %convolution_bitcast_fusion = f32[224,2048]{1,0:T(8,128)S(1)} fusion(bf16[3072,224]{0,1:T(8,128)(2,1)S(1)} %bitcast.136, bf16[3072,2048]{1,0:T(8,128)(2,1)} %all-gather.14.cloned.1.call-done), kind=kOutput, calls=%fused_computation.4 | convolution fusion | flops 2818572288 | bytes 15794176 | tf_op jit(solution)/shard_map/dot_general | solution.py:20
  285.1 20.5 %psum.14 = bf16[3,224,32]{1,2,0:T(8,128)(2,1)} all-reduce(bf16[3,224,32]{1,2,0:T(8,128)(2,1)} %pad_maximum_fusion.4), channel_id=1, replica_groups=mesh['node'=8,'grp'=4] {'grp'}, use_global_device_ids=true, to_apply=%region_0.0 | all-reduce | flops 21504 | bytes 86016 | tf_op jit(solution)/shard_map/psum | solution.py:64
  305.6 1.7 fusion.33
  307.3 1.4 convert_multiply_fusion
  308.8 24.0 %psum.15 = f32[3,32,32]{1,2,0:T(8,128)} all-reduce(f32[3,32,32]{1,2,0:T(8,128)} %fusion.33), channel_id=1, replica_groups=mesh['node'=8,'grp'=4] {'node'}, use_global_device_ids=true, to_apply=%region_1.0 | all-reduce | flops 3072 | bytes 24576 | tf_op jit(solution)/shard_map/psum | solution.py:66
  332.8 1.4 slice_bitcast_fusion.14
  335.0 1.4 copy.30
  336.3 1.4 copy.29
  337.7 1.4 fusion.39
  339.1 3.6 cholesky.59
  343.5 1.3 fusion.34
  344.7 3.8 custom-call.7
  348.5 3.6 cholesky.70
  352.8 1.3 fusion.35
  354.1 3.2 custom-call.8
  357.2 1.6 fusion.32
  358.8 1.6 fusion.31
  360.4 3.6 cholesky.81
  364.7 1.3 fusion.36
  366.0 3.2 custom-call.9
  369.1 1.0 fusion.30
  370.8 1.4 convolution_bitcast_fusion.3
  373.8 4.0 fusion.46
  377.9 2.7 fusion
  381.2 84.6 %all-gather.18.cloned.1.call-done = f32[96,1024,32]{1,2,0:T(8,128)} async-done(((f32[3,1024,32]{1,2,0:T(8,128)}), f32[96,1024,32]{1,2,0:T(8,128)}) %all-gather.18.cloned.1.call-update) | async-done | bytes 12582928 | tf_op jit(solution)/shard_map/all_gather | solution.py:72
  465.9 5.7 %reduce_sum.9 = f32[3,1024,32]{1,2,0:T(8,128)S(1)} reduce(f32[32,3,1024,32]{2,3,1,0:T(8,128)} %bitcast.132, f32[]{:T(128)} %constant.49.clone.1), dimensions={0}, to_apply=%region_4.7 | reduce | flops 3047424 | bytes 12976132 | tf_op jit(solution)/shard_map/reduce_sum | solution.py:72
  471.7 1.8 fusion.12
  473.4 0.9 fusion.13
  475.3 1.2 pad_maximum_fusion.1
  (63 shorter events, 14.0 us)
Async XLA Ops:
  7.2 39.8 %all-gather.8.cloned.1.call-start = ((), (), s32[]{:S(2)}) async-start(), calls=%async_computation.2 | async-start | bytes 4128768 | tf_op jit(solution)/shard_map/all_gather | solution.py:33
  7.9 75.4 %all-gather.12.cloned.1.call-start = ((), (), s32[]{:S(2)}) async-start(), calls=%async_computation.4 | async-start | bytes 4128768 | tf_op jit(solution)/shard_map/all_gather | solution.py:31
  8.6 111.0 %all-gather.10.cloned.1.call-start = ((), (), s32[]{:S(2)}) async-start(), calls=%async_computation.3 | async-start | bytes 4128768 | tf_op jit(solution)/shard_map/all_gather | solution.py:32
  9.4 73.9 %copy-start.2 = (bf16[384,1792]{1,0:T(8,128)(2,1)S(1)}, bf16[384,1792]{1,0:T(8,128)(2,1)}, u32[]{:S(2)}) copy-start(bf16[384,1792]{1,0:T(8,128)(2,1)} %param.10) | copy-start | bytes 4128772
  9.4 191.3 %all-gather.16.cloned.1.call-start = ((), (), s32[]{:S(2)}) async-start(), calls=%async_computation.6 | async-start | bytes 7077888 | tf_op jit(solution)/shard_map/all_gather | solution.py:56
  126.0 0.9 copy-start.7
  126.0 148.4 %all-gather.14.cloned.1.call-start = ((), (), s32[]{:S(2)}) async-start(), calls=%async_computation.5 | async-start | bytes 14155776 | tf_op jit(solution)/shard_map/all_gather | solution.py:55
  128.1 1.3 copy-start.1
  131.0 29.5 %all-to-all-start.1 = ((bf16[384,8,224]{0,2,1:T(8,128)(2,1)}), bf16[384,8,224]{0,2,1:T(8,128)(2,1)S(1)}, u32[]{:S(2)}, u32[]{:S(2)}) async-start(bf16[384,8,224]{0,2,1:T(8,128)(2,1)} %bitcast.3), calls=%async_computation.1 | async-start | bytes 2752512 | tf_op jit(solution)/shard_map/all_to_all | solution.py:53
  160.5 37.1 %all-to-all-start = ((bf16[384,8,224]{0,2,1:T(8,128)(2,1)}), bf16[384,8,224]{0,2,1:T(8,128)(2,1)S(1)}, u32[]{:S(2)}, u32[]{:S(2)}) async-start(bf16[384,8,224]{0,2,1:T(8,128)(2,1)} %bitcast), calls=%async_computation | async-start | bytes 2752512 | tf_op jit(solution)/shard_map/all_to_all | solution.py:52
  164.1 301.8 %all-gather.18.cloned.1.call-start = ((), (), s32[]{:S(2)}) async-start(), calls=%async_computation.7 | async-start | bytes 12976128 | tf_op jit(solution)/shard_map/all_gather | solution.py:72
  165.5 35.2 %copy-start.4 = (bf16[8,28,8,384]{3,2,0,1:T(8,128)(2,1)S(1)}, bf16[8,28,8,384]{3,2,0,1:T(8,128)(2,1)}, u32[]{:S(2)}) copy-start(bf16[8,28,8,384]{3,2,0,1:T(8,128)(2,1)} %copy.33) | copy-start | bytes 4128772
  200.6 73.8 %copy-start.5 = (bf16[8,28,8,384]{3,2,0,1:T(8,128)(2,1)S(1)}, bf16[8,28,8,384]{3,2,0,1:T(8,128)(2,1)}, u32[]{:S(2)}) copy-start(bf16[8,28,8,384]{3,2,0,1:T(8,128)(2,1)} %copy.32) | copy-start | bytes 4128772
  274.4 6.4 %copy-start.3 = (bf16[1,224,3072]{2,1,0:T(8,128)(2,1)S(1)}, bf16[1,224,3072]{2,1,0:T(8,128)(2,1)}, u32[]{:S(2)}) copy-start(bf16[1,224,3072]{2,1,0:T(8,128)(2,1)} %param.15) | copy-start | bytes 4128772
  274.4 6.4 %copy-start.6 = (f32[224,1024]{1,0:T(8,128)S(1)}, f32[224,1024]{1,0:T(8,128)}, u32[]{:S(2)}) copy-start(f32[224,1024]{1,0:T(8,128)} %convolution_bitcast_fusion.1) | copy-start | bytes 2752516
  280.8 1.0 copy-start.15
  369.1 3.1 copy-start.8
  370.2 2.8 copy-start.13
  373.8 4.1 copy-start.16
  377.8 2.7 copy-start.9
  377.9 2.7 copy-start.11
  377.9 2.7 copy-start.14
  471.6 1.8 copy-start.12
  471.6 3.7 copy-start
  471.6 2.7 copy-start.10
Sparse Core Ops, SparseCore 0:
  9.9 37.0 all-gather.7
  48.9 34.3 all-gather.11
  85.2 34.3 all-gather.9
  126.1 74.4 all-gather.15
  202.4 71.9 all-gather.13
  373.9 91.9 all-gather.17
